TPU v7x, 8 devices: a whole 2x2x1 slice. The times are simulated.
8 devices in a mesh: dp: 1 (over z), tp: 8 (over y, x, core).
Axes of the slice: x: 2, y: 2, z: 1, core: 2. Of those that a mesh axis runs over, the one named last changes fastest.
Arguments:
- x_norm: bfloat16 [256, 3072], P(('dp', 'tp'))
- w_gate: bfloat16 [3072, 8192], P(None, 'tp')
- w_up: bfloat16 [3072, 8192], P(None, 'tp')
- w_down: bfloat16 [8192, 3072], P('tp')
- u_gate: bfloat16 [256, 8192], P('dp', 'tp')
- u_up: bfloat16 [256, 8192], P('dp', 'tp')
- grad_out: bfloat16 [256, 3072], P(('dp', 'tp'))
Outputs:
- output 1: bfloat16 [256, 3072], P(('dp', 'tp'))
- output 2: float32 [3072, 8192], P('dp', 'tp')
- output 3: float32 [3072, 8192], P('dp', 'tp')
- output 4: float32 [8192, 3072], P(('dp', 'tp'))
All inputs are finite; a program needn't handle non-finite values.
Results may differ from a plain program's by a relative error of at most 0.0116367.
Values are sent between devices in bfloat16 or wider.
A program may use at most 1 GiB of HBM per device.

v0:
```python
import jax
import jax.numpy as jnp
from jax import lax
from jax.sharding import PartitionSpec as P

CONTRACT_ROWS = (((0,), (0,)), ((), ()))
CONTRACT_COLS = (((1,), (1,)), ((), ()))


def solution(mesh):
    def local_backward(x_loc, wg_loc, wu_loc, wd_loc, ug_loc, uu_loc, dy_loc):
        x_all = lax.all_gather(x_loc, 'tp', axis=0, tiled=True)
        dy_all = lax.all_gather(dy_loc, 'tp', axis=0, tiled=True)
        gate_pre = ug_loc.astype(jnp.float32)
        up_pre = uu_loc.astype(jnp.float32)
        sig_gate = jax.nn.sigmoid(gate_pre)
        gate_act = gate_pre * sig_gate
        z_act = (gate_act * up_pre).astype(jnp.bfloat16)
        grad_down = lax.dot_general(z_act, dy_all, CONTRACT_ROWS, preferred_element_type=jnp.float32)
        grad_hid = lax.dot_general(dy_all, wd_loc, CONTRACT_COLS, preferred_element_type=jnp.float32)
        grad_up = (grad_hid * gate_act).astype(jnp.bfloat16)
        grad_gate = (grad_hid * up_pre * sig_gate * (1.0 + gate_pre * (1.0 - sig_gate))).astype(jnp.bfloat16)
        part_x = (lax.dot_general(grad_gate, wg_loc, CONTRACT_COLS, preferred_element_type=jnp.float32)
                  + lax.dot_general(grad_up, wu_loc, CONTRACT_COLS, preferred_element_type=jnp.float32))
        grad_x = lax.psum_scatter(part_x.astype(jnp.bfloat16), 'tp', scatter_dimension=0, tiled=True)
        grad_wg = lax.dot_general(x_all, grad_gate, CONTRACT_ROWS, preferred_element_type=jnp.float32)
        grad_wu = lax.dot_general(x_all, grad_up, CONTRACT_ROWS, preferred_element_type=jnp.float32)
        return grad_x, grad_wg, grad_wu, grad_down

    tok_spec = P(('dp', 'tp'), None)
    col_spec = P(None, 'tp')
    act_spec = P('dp', 'tp')
    return jax.shard_map(local_backward, mesh=mesh,
                         in_specs=(tok_spec, col_spec, col_spec, P('tp', None), act_spec, act_spec, tok_spec),
                         out_specs=(tok_spec, act_spec, act_spec, tok_spec),
                         check_vma=False)
```

profile of v0, /device:TPU:0, one launch (start us, length us, event | category | flops | bytes accessed | tf_op | source)
XLA Modules:
  0.0 107.4 jit_solution(14987727232898401979)
XLA Ops:
  7.2 0.0 all-gather.3.cloned.1.call-start
  7.2 0.7 all-gather.3.cloned.1.call-update
  7.9 0.0 all-gather.5.cloned.1.call-start
  7.9 0.7 all-gather.5.cloned.1.call-update
  8.7 0.0 reduce-scatter.2.cloned.1.call-start
  8.7 23.7 %all-gather.3.cloned.1.call-done = bf16[256,3072]{1,0:T(8,128)(2,1)} async-done(((bf16[32,3072]{1,0:T(8,128)(2,1)}), bf16[256,3072]{1,0:T(8,128)(2,1)}) %all-gather.3.cloned.1.call-update) | async-done | bytes 1572880 | tf_op jit(solution)/shard_map/all_gather | solution.py:13
  32.4 5.5 %fusion.3 = (bf16[256,1024]{1,0:T(8,128)(2,1)S(1)}, f32[256,1024]{1,0:T(8,128)S(1)}) fusion(bf16[256,1024]{1,0:T(8,128)(2,1)} %param.12, bf16[256,1024]{1,0:T(8,128)(2,1)} %param.11, bf16[256,3072]{1,0:T(8,128)(2,1)} %all-gather.3.cloned.1.call-done, bf16[1024,3072]{1,0:T(8,128)(2,1)} %param.10), kind=kOutput, calls=%fused_computation.11 | convolution fusion | flops 1613758464 | bytes 10485760 | tf_op jit(solution)/shard_map/dot_general | solution.py:20
  37.9 0.0 copy-start.1
  37.9 0.0 copy-start.4
  38.0 4.8 %fusion.12 = f32[256,3072]{1,0:T(8,128)S(1)} fusion(bf16[256,1024]{1,0:T(8,128)(2,1)S(1)} %get-tuple-element.8, bf16[3072,1024]{1,0:T(8,128)(2,1)} %param.8), kind=kOutput, calls=%fused_computation.20 | convolution fusion | flops 1610612736 | bytes 9961472 | tf_op jit(solution)/shard_map/dot_general | solution.py:23
  42.7 0.0 copy-done.1
  42.7 0.0 copy-done.4
  42.7 3.1 %fusion = bf16[256,3072]{1,0:T(8,128)(2,1)} fusion(f32[256,3072]{1,0:T(8,128)S(1)} %fusion.12, bf16[3072,1024]{1,0:T(8,128)(2,1)S(1)} %copy-done.4, f32[256,1024]{1,0:T(8,128)S(1)} %get-tuple-element.9, bf16[256,1024]{1,0:T(8,128)(2,1)S(1)} %copy-done.1), kind=kOutput, calls=%fused_computation.3 | convolution fusion | flops 1614020608 | bytes 12582912 | tf_op jit(solution)/shard_map/dot_general | solution.py:24
  45.8 0.0 reduce-scatter.2.cloned.1.call-update
  45.9 8.1 %all-gather.5.cloned.1.call-done = bf16[256,3072]{1,0:T(8,128)(2,1)} async-done(((bf16[32,3072]{1,0:T(8,128)(2,1)}), bf16[256,3072]{1,0:T(8,128)(2,1)}) %all-gather.5.cloned.1.call-update) | async-done | bytes 1572880 | tf_op jit(solution)/shard_map/all_gather | solution.py:12
  54.0 8.0 %convolution_bitcast_fusion.1 = f32[3072,1024]{0,1:T(8,128)} fusion(bf16[256,1024]{1,0:T(8,128)(2,1)S(1)} %get-tuple-element.8, bf16[256,3072]{1,0:T(8,128)(2,1)} %all-gather.5.cloned.1.call-done), kind=kOutput, calls=%fused_computation.1 | convolution fusion | flops 1610612736 | bytes 14680064 | tf_op jit(solution)/shard_map/dot_general | solution.py:26
  62.0 0.0 copy-start
  62.0 12.7 %copy.11 = f32[3072,1024]{1,0:T(8,128)} copy(f32[3072,1024]{0,1:T(8,128)} %convolution_bitcast_fusion.1) | data formatting | bytes 25165824
  74.7 0.0 copy-done
  74.7 6.7 %convolution_bitcast_fusion = f32[3072,1024]{0,1:T(8,128)} fusion(bf16[256,3072]{1,0:T(8,128)(2,1)S(1)} %copy-done, f32[256,1024]{1,0:T(8,128)S(1)} %get-tuple-element.9, bf16[256,1024]{1,0:T(8,128)(2,1)S(1)} %copy-done.1), kind=kOutput, calls=%fused_computation | convolution fusion | flops 1612447744 | bytes 15728640 | tf_op jit(solution)/shard_map/dot_general | solution.py:27
  81.4 0.0 copy-start.2
  81.4 0.0 copy-start.3
  81.4 12.7 %copy.12 = f32[3072,1024]{1,0:T(8,128)} copy(f32[3072,1024]{0,1:T(8,128)} %convolution_bitcast_fusion) | data formatting | bytes 25165824
  94.2 0.0 copy-done.2
  94.2 0.0 copy-done.3
  94.2 6.7 %fusion.9 = f32[1024,3072]{1,0:T(8,128)} fusion(bf16[256,3072]{1,0:T(8,128)(2,1)S(1)} %copy-done.2, bf16[256,1024]{1,0:T(8,128)(2,1)S(1)} %copy-done.3, bf16[256,1024]{1,0:T(8,128)(2,1)S(1)} %copy-done.1), kind=kOutput, calls=%fused_computation.18 | convolution fusion | flops 1612709888 | bytes 15204352 | tf_op jit(solution)/shard_map/dot_general | solution.py:19
  100.9 0.0 reduce-scatter.2.cloned.1.call-done
Async XLA Ops:
  7.2 25.2 %all-gather.3.cloned.1.call-start = ((), (), s32[]{:S(2)}) async-start(), calls=%async_computation.1 | async-start | bytes 1769472 | tf_op jit(solution)/shard_map/all_gather | solution.py:13
  7.9 46.1 %all-gather.5.cloned.1.call-start = ((), (), s32[]{:S(2)}) async-start(), calls=%async_computation.3 | async-start | bytes 1769472 | tf_op jit(solution)/shard_map/all_gather | solution.py:12
  8.7 92.3 %reduce-scatter.2.cloned.1.call-start = ((), (), s32[]{:S(2)}) async-start(), calls=%async_computation.2 | async-start | bytes 1769472 | tf_op jit(solution)/shard_map/reduce_scatter | solution.py:25
  37.9 4.8 %copy-start.1 = (bf16[256,1024]{1,0:T(8,128)(2,1)S(1)}, bf16[256,1024]{1,0:T(8,128)(2,1)}, u32[]{:S(2)}) copy-start(bf16[256,1024]{1,0:T(8,128)(2,1)} %param.11) | copy-start | bytes 1572868
  37.9 4.8 %copy-start.4 = (bf16[3072,1024]{1,0:T(8,128)(2,1)S(1)}, bf16[3072,1024]{1,0:T(8,128)(2,1)}, u32[]{:S(2)}) copy-start(bf16[3072,1024]{1,0:T(8,128)(2,1)} %param.9) | copy-start | bytes 18874372
  62.0 12.7 %copy-start = (bf16[256,3072]{1,0:T(8,128)(2,1)S(1)}, bf16[256,3072]{1,0:T(8,128)(2,1)}, u32[]{:S(2)}) copy-start(bf16[256,3072]{1,0:T(8,128)(2,1)} %all-gather.5.cloned.1.call-done) | copy-start | bytes 4718596
  81.4 12.8 %copy-start.2 = (bf16[256,3072]{1,0:T(8,128)(2,1)S(1)}, bf16[256,3072]{1,0:T(8,128)(2,1)}, u32[]{:S(2)}) copy-start(bf16[256,3072]{1,0:T(8,128)(2,1)} %all-gather.3.cloned.1.call-done) | copy-start | bytes 4718596
  81.4 12.8 %copy-start.3 = (bf16[256,1024]{1,0:T(8,128)(2,1)S(1)}, bf16[256,1024]{1,0:T(8,128)(2,1)}, u32[]{:S(2)}) copy-start(bf16[256,1024]{1,0:T(8,128)(2,1)} %param.12) | copy-start | bytes 1572868
Sparse Core Ops, SparseCore 0:
  9.8 22.5 all-gather.2
  34.2 19.7 all-gather.4
  57.8 29.8 reduce-scatter.1
where the time goes:
time: 108 us; the launch traced here: 107 us
  matrix products  34.8 us (32%)
  waiting for transfers between devices  33.2 us (31%)
  local copies, waits for them, and re-layouts  25.5 us (24%)
  between operations  13.8 us (13%)
    unnamed x12, local copies, waits for them, and re-layouts  25.5 us
    all_gather x1, waiting for transfers between devices, local_backward(): dy_all = lax.all_gather(dy_loc, 'tp', axis=0, tiled=True)  23.7 us
    all_gather x1, waiting for transfers between devices, local_backward(): x_all = lax.all_gather(x_loc, 'tp', axis=0, tiled=True)  8.14 us
    dot_general x1, matrix products, local_backward(): lax.dot_general(x_all, grad_gate, CONTRACT_ROWS, preferred_element_type=j...  8.02 us
    dot_general x1, matrix products, local_backward(): lax.dot_general(z_act, dy_all, CONTRACT_ROWS, preferred_element_type=jnp....  6.74 us
    dot_general x1, matrix products, local_backward(): lax.dot_general(x_all, grad_up, CONTRACT_ROWS, preferred_element_type=jnp...  6.68 us
    dot_general x1, matrix products, local_backward(): lax.dot_general(dy_all, wd_loc, CONTRACT_COLS, preferred_element_type=jnp...  5.52 us
    dot_general x1, matrix products, local_backward(): lax.dot_general(grad_gate, wg_loc, CONTRACT_COLS, preferred_element_type=...  4.76 us
  transfers between devices with their start and end apart: 3, of which 2 were waited for; matrix products, arithmetic and copies ran while one was open for 56% of the time, Pallas kernels for 0%

commit v1 on v0

v1 whole, which is shorter than its diff:
```python
import jax
import jax.numpy as jnp
from jax import lax
from jax.experimental import pallas as pl
from jax.experimental.pallas import tpu as pltpu
from jax.sharding import PartitionSpec as P

CONTRACT_ROWS = (((0,), (0,)), ((), ()))
CONTRACT_COLS = (((1,), (1,)), ((), ()))
F32 = jnp.float32
BF16 = jnp.bfloat16
MIB = 2 ** 20

ROWS = 32
CHUNKS = 4
DX_CHUNK = 512
FROM_X, FROM_Y, FROM_D, FROM_P, PART_X, PART_Y, PART_D = range(7)
TO_X, TO_Y, TO_P, RELAY, FWD_X, FWD_Y, FWD_D = range(7)


def gather_kernel(x_in, dy_in, wg_in, wu_in, wd_in, ug_in, uu_in,
                  x_out, dy_out, z_out, dug_out, duu_out, own_out, px_out, py_out, pd_out,
                  x_all, dy_all, wg, wu, wd, ug, uu, act, slope, z, dug, duu, grad, part, mine, give, take, piece,
                  send_sem, recv_sem, give_sem, take_sem, load_sem, wd_sem, wg_sem, wu_sem, out_sem):
    me = lax.axis_index('tp')
    core = lax.rem(me, 2)
    chip = lax.div(me, 2)
    other = me + 1 - 2 * core
    step_x = 2 - 4 * lax.rem(chip, 2)
    step_y = 4 - 8 * lax.div(chip, 2)
    near_x, near_y, far = me + step_x, me + step_y, me + step_x + step_y
    p_x, p_y, p_d = other + step_x, other + step_y, other + step_x + step_y
    hidden = x_all.shape[1]
    width = hidden // CHUNKS
    n_dx = hidden // DX_CHUNK

    def block(buf, owner, c):
        return buf.at[pl.ds(pl.multiple_of(owner * ROWS, ROWS), ROWS), pl.ds(c * width, width)]

    def rows(buf, owner):
        return buf.at[pl.ds(pl.multiple_of(owner * ROWS, ROWS), ROWS), :]

    own_dy = pltpu.make_async_copy(dy_in, rows(dy_all, me), load_sem.at[0])
    own_x = pltpu.make_async_copy(x_in, rows(x_all, me), load_sem.at[1])
    get_ug = pltpu.make_async_copy(ug_in, ug, load_sem.at[2])
    get_uu = pltpu.make_async_copy(uu_in, uu, load_sem.at[3])
    own_dy.start()
    own_x.start()
    get_ug.start()
    get_uu.start()

    def wd_load(c):
        s = pl.ds(c * width, width)
        return pltpu.make_async_copy(wd_in.at[:, s], wd.at[:, s], wd_sem.at[c])

    def w_loads(h):
        s = pl.ds(h * DX_CHUNK, DX_CHUNK)
        return (pltpu.make_async_copy(wg_in.at[s, :], wg.at[s, :], wg_sem.at[h]),
                pltpu.make_async_copy(wu_in.at[s, :], wu.at[s, :], wu_sem.at[h]))

    for c in range(CHUNKS):
        wd_load(c).start()
    for h in range(n_dx):
        for load in w_loads(h):
            load.start()

    barrier = pltpu.get_barrier_semaphore()
    for peer in (other, near_x, near_y):
        pl.semaphore_signal(barrier, inc=1, device_id={'tp': peer}, device_id_type=pl.DeviceIdType.MESH)
    pl.semaphore_wait(barrier, 3)

    bufs = (dy_all, x_all)

    def copy(a, owner, c, to, send_kind, recv_kind):
        ref = block(bufs[a], owner, c)
        return pltpu.make_async_remote_copy(
            src_ref=ref, dst_ref=ref, send_sem=send_sem.at[a, send_kind, c], recv_sem=recv_sem.at[a, recv_kind, c],
            device_id={'tp': to}, device_id_type=pl.DeviceIdType.MESH)

    started = []

    def send(*args):
        cp = copy(*args)
        cp.start()
        started.append(cp)

    def arrived(a, owner, c, recv_kind):
        copy(a, owner, c, other, TO_P, recv_kind).wait_recv()

    half = CHUNKS // 2
    first = list(range(half))
    last = list(range(half, CHUNKS))

    def send_own(a):
        for c1, c2 in zip(first + last, last + first):
            send(a, me, c1, near_x, TO_X, FROM_X)
            send(a, me, c2, near_y, TO_Y, FROM_Y)
        for c in first + last:
            send(a, me, c, other, TO_P, FROM_P)

    def relay_step(a, i):
        c1, c2 = first[i], last[i]
        arrived(a, near_x, c1, FROM_X)
        send(a, near_x, c1, near_y, RELAY, FROM_D)
        send(a, near_x, c1, other, FWD_X, PART_X)
        arrived(a, near_y, c2, FROM_Y)
        send(a, near_y, c2, near_x, RELAY, FROM_D)
        send(a, near_y, c2, other, FWD_Y, PART_Y)

    def rest_step(a, i):
        c1, c2 = last[i], first[i]
        arrived(a, near_x, c1, FROM_X)
        send(a, near_x, c1, other, FWD_X, PART_X)
        arrived(a, near_y, c2, FROM_Y)
        send(a, near_y, c2, other, FWD_Y, PART_Y)

    def far_step(a, i):
        for c in (first[i], last[i]):
            arrived(a, far, c, FROM_D)
            send(a, far, c, other, FWD_D, PART_D)

    def partner_step(a, c):
        arrived(a, other, c, FROM_P)
        arrived(a, p_x, c, PART_X)
        arrived(a, p_y, c, PART_Y)
        arrived(a, p_d, c, PART_D)

    own_dy.wait()
    send_own(0)

    get_ug.wait()
    get_uu.wait()
    n_e = 8
    for r in range(n_e):
        s = pl.ds(r * (256 // n_e), 256 // n_e)
        gate = ug[s, :].astype(F32)
        sig = jax.nn.sigmoid(gate)
        a = gate * sig
        act[s, :] = a
        slope[s, :] = sig * (1.0 + gate * (1.0 - sig))
        z[s, :] = (a * uu[s, :].astype(F32)).astype(BF16)
    outs = [pltpu.make_async_copy(z, z_out, out_sem.at[0])]
    outs[-1].start()
    own_x.wait()

    for i in range(half):
        relay_step(0, i)
    send_own(1)
    for i in range(half):
        rest_step(0, i)

    fresh = True
    for i in range(half):
        far_step(0, i)
    for i in range(half):
        for c in (first[i], last[i]):
            partner_step(0, c)
            wd_load(c).wait()
            s = pl.ds(c * width, width)
            term = lax.dot_general(dy_all[:, s], wd[:, s], CONTRACT_COLS, preferred_element_type=F32)
            if fresh:
                grad[...] = term
            else:
                grad[...] += term
            fresh = False
    outs.append(pltpu.make_async_copy(dy_all, dy_out, out_sem.at[1]))
    outs[-1].start()

    for i in range(half):
        relay_step(1, i)
    for r in range(n_e):
        s = pl.ds(r * (256 // n_e), 256 // n_e)
        g = grad[s, :]
        duu[s, :] = (g * act[s, :]).astype(BF16)
        dug[s, :] = (g * uu[s, :].astype(F32) * slope[s, :]).astype(BF16)
    outs.append(pltpu.make_async_copy(dug, dug_out, out_sem.at[2]))
    outs[-1].start()
    outs.append(pltpu.make_async_copy(duu, duu_out, out_sem.at[3]))
    outs[-1].start()

    def give_copy(h):
        s = pl.ds(h * DX_CHUNK, DX_CHUNK)
        return pltpu.make_async_remote_copy(
            src_ref=give.at[:, s], dst_ref=take.at[:, s], send_sem=give_sem.at[h], recv_sem=take_sem.at[h],
            device_id={'tp': other}, device_id_type=pl.DeviceIdType.MESH)

    def combine(h):
        s = pl.ds(h * DX_CHUNK, DX_CHUNK)
        give_copy(h).wait_recv()
        piece[:, s] = (mine[:, s] + take[:, s].astype(F32)).astype(BF16)

    x_work = {1: lambda: rest_step(1, 0), 3: lambda: rest_step(1, 1), 4: lambda: far_step(1, 0)}
    for h in range(n_dx):
        for load in w_loads(h):
            load.wait()
        s = pl.ds(h * DX_CHUNK, DX_CHUNK)
        part[...] = (lax.dot_general(dug[...], wg[s, :], CONTRACT_COLS, preferred_element_type=F32)
                     + lax.dot_general(duu[...], wu[s, :], CONTRACT_COLS, preferred_element_type=F32))
        for j in range(4):
            d = pl.ds(j * ROWS, ROWS)
            give[d, s] = part[pl.ds(pl.multiple_of(j * 2 * ROWS + ROWS * (1 - core), ROWS), ROWS), :].astype(BF16)
            mine[d, s] = part[pl.ds(pl.multiple_of(j * 2 * ROWS + ROWS * core, ROWS), ROWS), :]
        give_copy(h).start()
        if h >= 2:
            combine(h - 2)
        if h in x_work:
            x_work[h]()
    far_step(1, 1)
    for h in range(n_dx - 2, n_dx):
        combine(h)
    for k, (ref, flip) in enumerate(((own_out, 0), (px_out, 1), (py_out, 2), (pd_out, 3))):
        fx, fy = flip % 2, flip // 2
        cx, cy = lax.rem(chip, 2), lax.div(chip, 2)
        to_chip = (cx + fx * (1 - 2 * cx)) + 2 * (cy + fy * (1 - 2 * cy))
        outs.append(pltpu.make_async_copy(
            piece.at[pl.ds(pl.multiple_of(to_chip * ROWS, ROWS), ROWS), :], ref, out_sem.at[4 + k]))
        outs[-1].start()
    for c in range(CHUNKS):
        partner_step(1, c)
    outs.append(pltpu.make_async_copy(x_all, x_out, out_sem.at[8]))
    outs[-1].start()
    for cp in started:
        cp.wait_send()
    for h in range(n_dx):
        give_copy(h).wait_send()
    for cp in outs:
        cp.wait()


def gather_call(x, dy, wg, wu, wd, ug, uu):
    hidden, f = wg.shape
    tokens = ug.shape[0]
    n_dx = hidden // DX_CHUNK
    any_spec = pl.BlockSpec(memory_space=pl.ANY)
    shape = jax.ShapeDtypeStruct
    full, act, row = shape((tokens, hidden), BF16), shape((tokens, f), BF16), shape((ROWS, hidden), BF16)
    dma = pltpu.SemaphoreType.DMA
    vmem = pltpu.VMEM
    return pl.pallas_call(
        gather_kernel,
        out_shape=(full, full, act, act, act, row, row, row, row),
        in_specs=[any_spec] * 7,
        out_specs=[any_spec] * 9,
        scratch_shapes=[
            vmem((tokens, hidden), BF16), vmem((tokens, hidden), BF16),
            vmem((hidden, f), BF16), vmem((hidden, f), BF16), vmem((f, hidden), BF16),
            vmem((tokens, f), BF16), vmem((tokens, f), BF16),
            vmem((tokens, f), F32), vmem((tokens, f), F32),
            vmem((tokens, f), BF16), vmem((tokens, f), BF16), vmem((tokens, f), BF16),
            vmem((tokens, f), F32), vmem((tokens, DX_CHUNK), F32),
            vmem((4 * ROWS, hidden), F32), vmem((4 * ROWS, hidden), BF16),
            vmem((4 * ROWS, hidden), BF16), vmem((4 * ROWS, hidden), BF16),
            dma((2, 7, CHUNKS)), dma((2, 7, CHUNKS)), dma((n_dx,)), dma((n_dx,)),
            dma((4,)), dma((CHUNKS,)), dma((n_dx,)), dma((n_dx,)), dma((9,)),
        ],
        compiler_params=pltpu.CompilerParams(collective_id=0, has_side_effects=True, vmem_limit_bytes=48 * MIB),
        cost_estimate=pl.CostEstimate(flops=6 * tokens * hidden * f, bytes_accessed=24 * MIB, transcendentals=0),
        name='gather_and_input_grad',
    )(x, dy, wg, wu, wd, ug, uu)


def weight_kernel(x, dy, z, dug, duu, dwg, dwu, dwd):
    xb = x[...]
    dwg[...] = lax.dot_general(xb, dug[...], CONTRACT_ROWS, preferred_element_type=F32)
    dwu[...] = lax.dot_general(xb, duu[...], CONTRACT_ROWS, preferred_element_type=F32)
    dwd[...] = lax.dot_general(z[...], dy[...], CONTRACT_ROWS, preferred_element_type=F32)


def weight_call(x, dy, z, dug, duu, steps=12):
    tokens, hidden = x.shape
    f = z.shape[1]
    h = hidden // steps
    cols = pl.BlockSpec((tokens, h), lambda i: (0, i))
    whole = pl.BlockSpec((tokens, f), lambda i: (0, 0))
    tall = pl.BlockSpec((h, f), lambda i: (i, 0))
    wide = pl.BlockSpec((f, h), lambda i: (0, i))
    return pl.pallas_call(
        weight_kernel,
        grid=(steps,),
        in_specs=[cols, cols, whole, whole, whole],
        out_specs=[tall, tall, wide],
        out_shape=(jax.ShapeDtypeStruct((hidden, f), F32), jax.ShapeDtypeStruct((hidden, f), F32),
                   jax.ShapeDtypeStruct((f, hidden), F32)),
        compiler_params=pltpu.CompilerParams(vmem_limit_bytes=40 * MIB),
        cost_estimate=pl.CostEstimate(flops=6 * tokens * hidden * f, bytes_accessed=42 * MIB, transcendentals=0),
        name='weight_grads',
    )(x, dy, z, dug, duu)


def solution(mesh):
    n = mesh.shape['tp']

    def local_backward(x, wg, wu, wd, ug, uu, dy):
        x_all, dy_all, z, dug, duu, own, px, py, pd = gather_call(x, dy, wg, wu, wd, ug, uu)

        def swap(v, k):
            return lax.ppermute(v, 'tp', [(i, i ^ k) for i in range(n)])

        rx, ry, rd = swap(px, 2), swap(py, 4), swap(pd, 6)
        dwg, dwu, dwd = weight_call(x_all, dy_all, z, dug, duu)
        dx = (own.astype(F32) + rx.astype(F32) + ry.astype(F32) + rd.astype(F32)).astype(BF16)
        return dx, dwg, dwu, dwd

    tok_spec = P(('dp', 'tp'), None)
    col_spec = P(None, 'tp')
    act_spec = P('dp', 'tp')
    return jax.shard_map(local_backward, mesh=mesh,
                         in_specs=(tok_spec, col_spec, col_spec, P('tp', None), act_spec, act_spec, tok_spec),
                         out_specs=(tok_spec, act_spec, act_spec, tok_spec),
                         check_vma=False)
```

time: 108 us -> 48 us (0.44)
  Pallas kernels: 0 us -> 37.5 us
  matrix products: 34.8 us -> 0 us
  waiting for transfers between devices: 33.2 us -> 0.01 us
  local copies, waits for them, and re-layouts: 25.5 us -> 5.34 us
  between operations: 13.8 us -> 0.66 us
  starting transfers between devices: 0.11 us -> 3.51 us
    pallas_call x0 -> x2, Pallas kernels: none -> 37.5 us  [the longest x1 24.5 us: gather_call(): pl.pallas_call(gather_kernel, out_shape=(full, full, act, act, act, row,...]
    dot_general x6 -> x0, matrix products: 34.8 us -> none  [the longest x1 8.02 us: local_backward(): lax.dot_general(x_all, grad_gate, CONTRACT_ROWS, preferred_element_type=j...]
    all_gather x2 -> x0, waiting for transfers between devices: 31.8 us -> none  [the longest x1 23.7 us: local_backward(): dy_all = lax.all_gather(dy_loc, 'tp', axis=0, tiled=True)]
    unnamed x12 -> x10, local copies, waits for them, and re-layouts: 25.5 us -> 5.34 us
    ppermute x0 -> x3, starting transfers between devices: none -> 3.51 us  [swap(): return lax.ppermute(v, 'tp', [(i, i ^ k) for i in range(n)])]
    unnamed x3 -> x0, waiting for transfers between devices: 1.39 us -> none
  transfers between devices with their start and end apart: 3 -> 3, of which waited for: 2 -> 0; matrix products, arithmetic and copies ran while one was open for 56% -> 0% of each run, Pallas kernels for 0% -> 27%
where the time goes in v1:
time: 48 us; the launch traced here: 47.8 us
  Pallas kernels  37.5 us (78%)
  local copies, waits for them, and re-layouts  5.34 us (11%)
  starting transfers between devices  3.51 us (7%)
  other arithmetic  0.78 us (2%)
  between operations  0.66 us (1%)
    pallas_call x1, Pallas kernels, gather_call(): pl.pallas_call(gather_kernel, out_shape=(full, full, act, act, act, row,...  24.5 us
    pallas_call x1, Pallas kernels, weight_call(): pl.pallas_call(weight_kernel, grid=(steps,), in_specs=[cols, cols, whole,...  13 us
    unnamed x10, local copies, waits for them, and re-layouts  5.34 us
    ppermute x3, starting transfers between devices, swap(): return lax.ppermute(v, 'tp', [(i, i ^ k) for i in range(n)])  3.51 us
  transfers between devices with their start and end apart: 3, of which 0 were waited for; matrix products, arithmetic and copies ran while one was open for 0% of the time, Pallas kernels for 27%

profile of v1, /device:TPU:0, one launch (start us, length us, event | category | flops | bytes accessed | tf_op | source)
XLA Modules:
  0.0 47.8 jit_solution(994615336948001102)
XLA Ops:
  0.6 0.0 copy-start
  0.6 1.0 %copy-done = bf16[256,1024]{1,0:T(8,128)(2,1)S(1)} copy-done((bf16[256,1024]{1,0:T(8,128)(2,1)S(1)}, bf16[256,1024]{1,0:T(8,128)(2,1)}, u32[]{:S(2)}) %copy-start) | copy-done | bytes 524312
  1.7 0.0 copy-start.1
  1.7 1.0 %copy-done.1 = bf16[256,1024]{1,0:T(8,128)(2,1)S(1)} copy-done((bf16[256,1024]{1,0:T(8,128)(2,1)S(1)}, bf16[256,1024]{1,0:T(8,128)(2,1)}, u32[]{:S(2)}) %copy-start.1) | copy-done | bytes 524312
  2.7 0.0 copy-start.2
  2.7 0.9 %copy-done.2 = bf16[32,3072]{1,0:T(8,128)(2,1)S(1)} copy-done((bf16[32,3072]{1,0:T(8,128)(2,1)S(1)}, bf16[32,3072]{1,0:T(8,128)(2,1)}, u32[]{:S(2)}) %copy-start.2) | copy-done | bytes 196632
  3.6 0.0 copy-start.3
  3.6 0.9 %copy-done.3 = bf16[32,3072]{1,0:T(8,128)(2,1)S(1)} copy-done((bf16[32,3072]{1,0:T(8,128)(2,1)S(1)}, bf16[32,3072]{1,0:T(8,128)(2,1)}, u32[]{:S(2)}) %copy-start.3) | copy-done | bytes 196632
  4.6 24.5 %gather_and_input_grad.1 = (bf16[256,3072]{1,0:T(8,128)(2,1)S(1)}, bf16[256,3072]{1,0:T(8,128)(2,1)}, bf16[256,1024]{1,0:T(8,128)(2,1)S(1)}, bf16[256,1024]{1,0:...) custom-call(bf16[32,3072]{1,0:T(8,128)(2,1)S(1)} %copy-done.2, ...), custom_call_target="tpu_custom_call" | custom-call | flops 4831838208 | bytes 25165824 | tf_op jit(solution)/shard_map/gather_and_input_grad/pallas_call | solution.py:239
  29.1 0.6 %collective-permute-start = (bf16[32,3072]{1,0:T(8,128)(2,1)S(1)}, bf16[32,3072]{1,0:T(8,128)(2,1)S(1)}, u32[]{:S(2)}, u32[]{:S(2)}) collective-permute-start(bf16[32,3072]{1,0:T(8,128)(2,1)S(1)} %get-tuple-element.17), channel_id=1, source_target_pairs={{0,2},{1,3},{2,0},{3,1},{4,6},{5,7},{6,4},{7,5}} | collective-permute-start | bytes 589832 | tf_op jit(solution)/shard_map/ppermute | solution.py:297
  29.6 1.5 %collective-permute-start.1 = (bf16[32,3072]{1,0:T(8,128)(2,1)S(1)}, bf16[32,3072]{1,0:T(8,128)(2,1)S(1)}, u32[]{:S(2)}, u32[]{:S(2)}) collective-permute-start(bf16[32,3072]{1,0:T(8,128)(2,1)S(1)} %get-tuple-element.18), channel_id=1, source_target_pairs={{0,4},{1,5},{2,6},{3,7},{4,0},{5,1},{6,2},{7,3}} | collective-permute-start | bytes 589832 | tf_op jit(solution)/shard_map/ppermute | solution.py:297
  31.1 1.5 %collective-permute-start.2 = (bf16[32,3072]{1,0:T(8,128)(2,1)S(1)}, bf16[32,3072]{1,0:T(8,128)(2,1)S(1)}, u32[]{:S(2)}, u32[]{:S(2)}) collective-permute-start(bf16[32,3072]{1,0:T(8,128)(2,1)S(1)} %get-tuple-element.19), channel_id=1, source_target_pairs={{0,6},{1,7},{2,4},{3,5},{4,2},{5,3},{6,0},{7,1}} | collective-permute-start | bytes 589832 | tf_op jit(solution)/shard_map/ppermute | solution.py:297
  32.6 0.0 copy-start.4
  32.6 1.4 %copy-done.4 = bf16[256,3072]{1,0:T(8,128)(2,1)S(1)} copy-done((bf16[256,3072]{1,0:T(8,128)(2,1)S(1)}, bf16[256,3072]{1,0:T(8,128)(2,1)}, u32[]{:S(2)}) %copy-start.4) | copy-done | bytes 1572888
  34.0 13.0 %weight_grads.1 = (f32[3072,1024]{1,0:T(8,128)}, f32[3072,1024]{1,0:T(8,128)}, f32[1024,3072]{1,0:T(8,128)}) custom-call(bf16[256,3072]{1,0:T(8,128)(2,1)S(1)} %get-tuple-element.20.x, bf16[256,3072]{1,0:T(8,128)(2,1)S(1)} %copy-done.4, bf16[256,1024]{1,0:T(8,128)(2,1)S(1)} %get-tuple-element.22.z, bf16[256,1024]{1,0:T(8,128)(2,1)S(1)} %get-tuple-element.23.dug, ...), custom_call_target="tpu_custom_call" | custom-call | flops 4831838208 | bytes 44040192 | tf_op jit(solution)/shard_map/weight_grads/pallas_call | solution.py:277
  47.0 0.0 collective-permute-done
  47.0 0.0 collective-permute-done.1
  47.0 0.0 collective-permute-done.2
  47.0 0.8 %add_convert_fusion = bf16[32,3072]{1,0:T(8,128)(2,1)} fusion(bf16[32,3072]{1,0:T(8,128)(2,1)S(1)} %collective-permute-done.2, bf16[32,3072]{1,0:T(8,128)(2,1)S(1)} %collective-permute-done.1, bf16[32,3072]{1,0:T(8,128)(2,1)S(1)} %collective-permute-done, bf16[32,3072]{1,0:T(8,128)(2,1)S(1)} %get-tuple-element.16), kind=kLoop, calls=%fused_computation | loop fusion | flops 786432 | bytes 983040 | tf_op jit(solution)/shard_map/convert_element_type | solution.py:301
Async XLA Ops:
  0.6 1.0 %copy-start = (bf16[256,1024]{1,0:T(8,128)(2,1)S(1)}, bf16[256,1024]{1,0:T(8,128)(2,1)}, u32[]{:S(2)}) copy-start(bf16[256,1024]{1,0:T(8,128)(2,1)} %ug_in.1) | copy-start | bytes 1572868
  1.7 1.0 %copy-start.1 = (bf16[256,1024]{1,0:T(8,128)(2,1)S(1)}, bf16[256,1024]{1,0:T(8,128)(2,1)}, u32[]{:S(2)}) copy-start(bf16[256,1024]{1,0:T(8,128)(2,1)} %uu_in.1) | copy-start | bytes 1572868
  2.7 0.9 %copy-start.2 = (bf16[32,3072]{1,0:T(8,128)(2,1)S(1)}, bf16[32,3072]{1,0:T(8,128)(2,1)}, u32[]{:S(2)}) copy-start(bf16[32,3072]{1,0:T(8,128)(2,1)} %x_in.1) | copy-start | bytes 589828
  3.6 0.9 %copy-start.3 = (bf16[32,3072]{1,0:T(8,128)(2,1)S(1)}, bf16[32,3072]{1,0:T(8,128)(2,1)}, u32[]{:S(2)}) copy-start(bf16[32,3072]{1,0:T(8,128)(2,1)} %dy_in.1) | copy-start | bytes 589828
  29.1 17.9 %collective-permute-start = (bf16[32,3072]{1,0:T(8,128)(2,1)S(1)}, bf16[32,3072]{1,0:T(8,128)(2,1)S(1)}, u32[]{:S(2)}, u32[]{:S(2)}) collective-permute-start(bf16[32,3072]{1,0:T(8,128)(2,1)S(1)} %get-tuple-element.17), channel_id=1, source_target_pairs={{0,2},{1,3},{2,0},{3,1},{4,6},{5,7},{6,4},{7,5}} | collective-permute-start | bytes 589832 | tf_op jit(solution)/shard_map/ppermute | solution.py:297
  29.6 17.3 %collective-permute-start.1 = (bf16[32,3072]{1,0:T(8,128)(2,1)S(1)}, bf16[32,3072]{1,0:T(8,128)(2,1)S(1)}, u32[]{:S(2)}, u32[]{:S(2)}) collective-permute-start(bf16[32,3072]{1,0:T(8,128)(2,1)S(1)} %get-tuple-element.18), channel_id=1, source_target_pairs={{0,4},{1,5},{2,6},{3,7},{4,0},{5,1},{6,2},{7,3}} | collective-permute-start | bytes 589832 | tf_op jit(solution)/shard_map/ppermute | solution.py:297
  31.1 15.9 %collective-permute-start.2 = (bf16[32,3072]{1,0:T(8,128)(2,1)S(1)}, bf16[32,3072]{1,0:T(8,128)(2,1)S(1)}, u32[]{:S(2)}, u32[]{:S(2)}) collective-permute-start(bf16[32,3072]{1,0:T(8,128)(2,1)S(1)} %get-tuple-element.19), channel_id=1, source_target_pairs={{0,6},{1,7},{2,4},{3,5},{4,2},{5,3},{6,0},{7,1}} | collective-permute-start | bytes 589832 | tf_op jit(solution)/shard_map/ppermute | solution.py:297
  32.6 1.4 %copy-start.4 = (bf16[256,3072]{1,0:T(8,128)(2,1)S(1)}, bf16[256,3072]{1,0:T(8,128)(2,1)}, u32[]{:S(2)}) copy-start(bf16[256,3072]{1,0:T(8,128)(2,1)} %get-tuple-element.21.dy) | copy-start | bytes 4718596

commit v2 on v1

--- a/solution.py
+++ b/solution.py
@@ -19,9 +19,9 @@
 
 
 def gather_kernel(x_in, dy_in, wg_in, wu_in, wd_in, ug_in, uu_in,
-                  x_out, dy_out, z_out, dug_out, duu_out, own_out, px_out, py_out, pd_out,
-                  x_all, dy_all, wg, wu, wd, ug, uu, act, slope, z, dug, duu, grad, part, mine, give, take, piece,
-                  send_sem, recv_sem, give_sem, take_sem, load_sem, wd_sem, wg_sem, wu_sem, out_sem):
+                  x_all, dy_all, z, dug, duu, own_out, px_out, py_out, pd_out,
+                  wg, wu, wd, ug, uu, act, slope, grad, part, mine, give, take,
+                  send_sem, recv_sem, give_sem, take_sem, load_sem, wd_sem, wg_sem, wu_sem):
     me = lax.axis_index('tp')
     core = lax.rem(me, 2)
     chip = lax.div(me, 2)
@@ -139,8 +139,6 @@
         act[s, :] = a
         slope[s, :] = sig * (1.0 + gate * (1.0 - sig))
         z[s, :] = (a * uu[s, :].astype(F32)).astype(BF16)
-    outs = [pltpu.make_async_copy(z, z_out, out_sem.at[0])]
-    outs[-1].start()
     own_x.wait()
 
     for i in range(half):
@@ -163,8 +161,6 @@
             else:
                 grad[...] += term
             fresh = False
-    outs.append(pltpu.make_async_copy(dy_all, dy_out, out_sem.at[1]))
-    outs[-1].start()
 
     for i in range(half):
         relay_step(1, i)
@@ -173,10 +169,6 @@
         g = grad[s, :]
         duu[s, :] = (g * act[s, :]).astype(BF16)
         dug[s, :] = (g * uu[s, :].astype(F32) * slope[s, :]).astype(BF16)
-    outs.append(pltpu.make_async_copy(dug, dug_out, out_sem.at[2]))
-    outs[-1].start()
-    outs.append(pltpu.make_async_copy(duu, duu_out, out_sem.at[3]))
-    outs[-1].start()
 
     def give_copy(h):
         s = pl.ds(h * DX_CHUNK, DX_CHUNK)
@@ -187,7 +179,10 @@
     def combine(h):
         s = pl.ds(h * DX_CHUNK, DX_CHUNK)
         give_copy(h).wait_recv()
-        piece[:, s] = (mine[:, s] + take[:, s].astype(F32)).astype(BF16)
+        for ref, to_chip in ((own_out, chip), (px_out, lax.div(near_x, 2)), (py_out, lax.div(near_y, 2)),
+                             (pd_out, lax.div(far, 2))):
+            d = pl.ds(pl.multiple_of(to_chip * ROWS, ROWS), ROWS)
+            ref[:, s] = (mine[d, s] + take[d, s].astype(F32)).astype(BF16)
 
     x_work = {1: lambda: rest_step(1, 0), 3: lambda: rest_step(1, 1), 4: lambda: far_step(1, 0)}
     for h in range(n_dx):
@@ -208,23 +203,12 @@
     far_step(1, 1)
     for h in range(n_dx - 2, n_dx):
         combine(h)
-    for k, (ref, flip) in enumerate(((own_out, 0), (px_out, 1), (py_out, 2), (pd_out, 3))):
-        fx, fy = flip % 2, flip // 2
-        cx, cy = lax.rem(chip, 2), lax.div(chip, 2)
-        to_chip = (cx + fx * (1 - 2 * cx)) + 2 * (cy + fy * (1 - 2 * cy))
-        outs.append(pltpu.make_async_copy(
-            piece.at[pl.ds(pl.multiple_of(to_chip * ROWS, ROWS), ROWS), :], ref, out_sem.at[4 + k]))
-        outs[-1].start()
     for c in range(CHUNKS):
         partner_step(1, c)
-    outs.append(pltpu.make_async_copy(x_all, x_out, out_sem.at[8]))
-    outs[-1].start()
     for cp in started:
         cp.wait_send()
     for h in range(n_dx):
         give_copy(h).wait_send()
-    for cp in outs:
-        cp.wait()
 
 
 def gather_call(x, dy, wg, wu, wd, ug, uu):
@@ -232,26 +216,24 @@
     tokens = ug.shape[0]
     n_dx = hidden // DX_CHUNK
     any_spec = pl.BlockSpec(memory_space=pl.ANY)
-    shape = jax.ShapeDtypeStruct
-    full, act, row = shape((tokens, hidden), BF16), shape((tokens, f), BF16), shape((ROWS, hidden), BF16)
+    x, dy, wg, wu, wd, ug, uu = [pltpu.with_memory_space_constraint(v, pltpu.HBM) for v in (x, dy, wg, wu, wd, ug, uu)]
+    vmem = pltpu.VMEM
+    full, act, row = vmem((tokens, hidden), BF16), vmem((tokens, f), BF16), vmem((ROWS, hidden), BF16)
     dma = pltpu.SemaphoreType.DMA
-    vmem = pltpu.VMEM
     return pl.pallas_call(
         gather_kernel,
         out_shape=(full, full, act, act, act, row, row, row, row),
         in_specs=[any_spec] * 7,
-        out_specs=[any_spec] * 9,
+        out_specs=[pl.BlockSpec(memory_space=vmem)] * 9,
         scratch_shapes=[
-            vmem((tokens, hidden), BF16), vmem((tokens, hidden), BF16),
             vmem((hidden, f), BF16), vmem((hidden, f), BF16), vmem((f, hidden), BF16),
             vmem((tokens, f), BF16), vmem((tokens, f), BF16),
             vmem((tokens, f), F32), vmem((tokens, f), F32),
-            vmem((tokens, f), BF16), vmem((tokens, f), BF16), vmem((tokens, f), BF16),
             vmem((tokens, f), F32), vmem((tokens, DX_CHUNK), F32),
             vmem((4 * ROWS, hidden), F32), vmem((4 * ROWS, hidden), BF16),
-            vmem((4 * ROWS, hidden), BF16), vmem((4 * ROWS, hidden), BF16),
+            vmem((4 * ROWS, hidden), BF16),
             dma((2, 7, CHUNKS)), dma((2, 7, CHUNKS)), dma((n_dx,)), dma((n_dx,)),
-            dma((4,)), dma((CHUNKS,)), dma((n_dx,)), dma((n_dx,)), dma((9,)),
+            dma((4,)), dma((CHUNKS,)), dma((n_dx,)), dma((n_dx,)),
         ],
         compiler_params=pltpu.CompilerParams(collective_id=0, has_side_effects=True, vmem_limit_bytes=48 * MIB),
         cost_estimate=pl.CostEstimate(flops=6 * tokens * hidden * f, bytes_accessed=24 * MIB, transcendentals=0),

time: 48 us -> 42.1 us (0.88)
  local copies, waits for them, and re-layouts: 5.34 us -> 0 us
  Pallas kernels: 37.5 us -> 37 us
    unnamed x10 -> x0, local copies, waits for them, and re-layouts: 5.34 us -> none
    pallas_call x1, Pallas kernels: 24.5 us -> 24 us  [gather_call(): pl.pallas_call(gather_kernel, out_shape=(full, full, act, act, act, row,...]
  transfers between devices with their start and end apart: 3 -> 3, of which waited for: 0 -> 0; matrix products, arithmetic and copies ran while one was open for 0% -> 0% of each run, Pallas kernels for 27% -> 31%
where the time goes in v2:
time: 42.1 us; the launch traced here: 42 us
  Pallas kernels  37 us (88%)
  starting transfers between devices  3.51 us (8%)
  other arithmetic  0.78 us (2%)
  between operations  0.65 us (2%)
    pallas_call x1, Pallas kernels, gather_call(): pl.pallas_call(gather_kernel, out_shape=(full, full, act, act, act, row,...  24 us
    pallas_call x1, Pallas kernels, weight_call(): pl.pallas_call(weight_kernel, grid=(steps,), in_specs=[cols, cols, whole,...  13 us
    ppermute x3, starting transfers between devices, swap(): return lax.ppermute(v, 'tp', [(i, i ^ k) for i in range(n)])  3.51 us
  transfers between devices with their start and end apart: 3, of which 0 were waited for; matrix products, arithmetic and copies ran while one was open for 0% of the time, Pallas kernels for 31%

profile of v2, /device:TPU:0, one launch (start us, length us, event | category | flops | bytes accessed | tf_op | source)
XLA Modules:
  0.0 42.0 jit_solution(173844789005619446)
XLA Ops:
  0.6 24.0 %gather_and_input_grad.1 = (bf16[256,3072]{1,0:T(8,128)(2,1)S(1)}, bf16[256,3072]{1,0:T(8,128)(2,1)S(1)}, bf16[256,1024]{1,0:T(8,128)(2,1)S(1)}, bf16[256,1024]{...) custom-call(bf16[32,3072]{1,0:T(8,128)(2,1)} %x_in.1, ...), custom_call_target="tpu_custom_call" | custom-call | flops 4831838208 | bytes 25165824 | tf_op jit(solution)/shard_map/gather_and_input_grad/pallas_call | solution.py:223
  24.7 1.5 %collective-permute-start = (bf16[32,3072]{1,0:T(8,128)(2,1)S(1)}, bf16[32,3072]{1,0:T(8,128)(2,1)S(1)}, u32[]{:S(2)}, u32[]{:S(2)}) collective-permute-start(bf16[32,3072]{1,0:T(8,128)(2,1)S(1)} %get-tuple-element.17), channel_id=1, source_target_pairs={{0,2},{1,3},{2,0},{3,1},{4,6},{5,7},{6,4},{7,5}} | collective-permute-start | bytes 589832 | tf_op jit(solution)/shard_map/ppermute | solution.py:279
  26.2 0.5 %collective-permute-start.1 = (bf16[32,3072]{1,0:T(8,128)(2,1)S(1)}, bf16[32,3072]{1,0:T(8,128)(2,1)S(1)}, u32[]{:S(2)}, u32[]{:S(2)}) collective-permute-start(bf16[32,3072]{1,0:T(8,128)(2,1)S(1)} %get-tuple-element.18), channel_id=1, source_target_pairs={{0,4},{1,5},{2,6},{3,7},{4,0},{5,1},{6,2},{7,3}} | collective-permute-start | bytes 589832 | tf_op jit(solution)/shard_map/ppermute | solution.py:279
  26.7 1.5 %collective-permute-start.2 = (bf16[32,3072]{1,0:T(8,128)(2,1)S(1)}, bf16[32,3072]{1,0:T(8,128)(2,1)S(1)}, u32[]{:S(2)}, u32[]{:S(2)}) collective-permute-start(bf16[32,3072]{1,0:T(8,128)(2,1)S(1)} %get-tuple-element.19), channel_id=1, source_target_pairs={{0,6},{1,7},{2,4},{3,5},{4,2},{5,3},{6,0},{7,1}} | collective-permute-start | bytes 589832 | tf_op jit(solution)/shard_map/ppermute | solution.py:279
  28.2 13.0 %weight_grads.1 = (f32[3072,1024]{1,0:T(8,128)}, f32[3072,1024]{1,0:T(8,128)}, f32[1024,3072]{1,0:T(8,128)}) custom-call(bf16[256,3072]{1,0:T(8,128)(2,1)S(1)} %get-tuple-element.20.x, bf16[256,3072]{1,0:T(8,128)(2,1)S(1)} %get-tuple-element.21.dy, bf16[256,1024]{1,0:T(8,128)(2,1)S(1)} %get-tuple-element.22.z, bf16[256,1024]{1,0:T(8,128)(2,1)S(1)} %get-tuple-element.23.dug, ...), custom_call_target="tpu_custom_call" | custom-call | flops 4831838208 | bytes 44040192 | tf_op jit(solution)/shard_map/weight_grads/pallas_call | solution.py:259
  41.2 0.0 collective-permute-done
  41.2 0.0 collective-permute-done.1
  41.2 0.0 collective-permute-done.2
  41.2 0.8 %add_convert_fusion = bf16[32,3072]{1,0:T(8,128)(2,1)} fusion(bf16[32,3072]{1,0:T(8,128)(2,1)S(1)} %collective-permute-done.2, bf16[32,3072]{1,0:T(8,128)(2,1)S(1)} %collective-permute-done.1, bf16[32,3072]{1,0:T(8,128)(2,1)S(1)} %collective-permute-done, bf16[32,3072]{1,0:T(8,128)(2,1)S(1)} %get-tuple-element.16), kind=kLoop, calls=%fused_computation | loop fusion | flops 786432 | bytes 983040 | tf_op jit(solution)/shard_map/convert_element_type | solution.py:283
Async XLA Ops:
  24.7 16.5 %collective-permute-start = (bf16[32,3072]{1,0:T(8,128)(2,1)S(1)}, bf16[32,3072]{1,0:T(8,128)(2,1)S(1)}, u32[]{:S(2)}, u32[]{:S(2)}) collective-permute-start(bf16[32,3072]{1,0:T(8,128)(2,1)S(1)} %get-tuple-element.17), channel_id=1, source_target_pairs={{0,2},{1,3},{2,0},{3,1},{4,6},{5,7},{6,4},{7,5}} | collective-permute-start | bytes 589832 | tf_op jit(solution)/shard_map/ppermute | solution.py:279
  26.2 15.0 %collective-permute-start.1 = (bf16[32,3072]{1,0:T(8,128)(2,1)S(1)}, bf16[32,3072]{1,0:T(8,128)(2,1)S(1)}, u32[]{:S(2)}, u32[]{:S(2)}) collective-permute-start(bf16[32,3072]{1,0:T(8,128)(2,1)S(1)} %get-tuple-element.18), channel_id=1, source_target_pairs={{0,4},{1,5},{2,6},{3,7},{4,0},{5,1},{6,2},{7,3}} | collective-permute-start | bytes 589832 | tf_op jit(solution)/shard_map/ppermute | solution.py:279
  26.7 14.5 %collective-permute-start.2 = (bf16[32,3072]{1,0:T(8,128)(2,1)S(1)}, bf16[32,3072]{1,0:T(8,128)(2,1)S(1)}, u32[]{:S(2)}, u32[]{:S(2)}) collective-permute-start(bf16[32,3072]{1,0:T(8,128)(2,1)S(1)} %get-tuple-element.19), channel_id=1, source_target_pairs={{0,6},{1,7},{2,4},{3,5},{4,2},{5,3},{6,0},{7,1}} | collective-permute-start | bytes 589832 | tf_op jit(solution)/shard_map/ppermute | solution.py:279

commit v3 on v0

v3 whole, which is shorter than its diff:
```python
import jax
import jax.numpy as jnp
from jax import lax
from jax.experimental import pallas as pl
from jax.experimental.pallas import tpu as pltpu
from jax.sharding import PartitionSpec as P

CONTRACT_ROWS = (((0,), (0,)), ((), ()))
CONTRACT_COLS = (((1,), (1,)), ((), ()))
F32 = jnp.float32
BF16 = jnp.bfloat16
MIB = 2 ** 20

ROWS = 32
DY_CHUNKS = 4
X_CHUNKS = 2
DX_CHUNK = 1024
E_BLOCKS = 8
MESH = pl.DeviceIdType.MESH


def gather_kernel(x_in, dy_in, wg_in, wu_in, wd_in, ug_in, uu_in,
                  x_all, dy_all, z, dug, duu, own_out, px_out, py_out, pd_out,
                  wgu, wd, ugu, act, slope, grad, part, mine, give, take,
                  dy_x, dy_y, dy_d, dy_p, x_x, x_y, x_d, x_p, sent, give_sem, take_sem, own_sem, load_sem):
    me = lax.axis_index('tp')
    core = lax.rem(me, 2)
    chip = lax.div(me, 2)
    other = me + 1 - 2 * core
    step_x = 2 - 4 * lax.rem(chip, 2)
    step_y = 4 - 8 * lax.div(chip, 2)
    near_x, near_y, far = me + step_x, me + step_y, me + step_x + step_y
    tokens, hidden = x_all.shape
    f = dug.shape[1]
    n_dx = hidden // DX_CHUNK

    def rows(buf, owner):
        return buf.at[pl.ds(pl.multiple_of(owner * ROWS, ROWS), ROWS), :]

    own_dy = pltpu.make_async_copy(dy_in, rows(dy_all, me), own_sem.at[0])
    own_x = pltpu.make_async_copy(x_in, rows(x_all, me), own_sem.at[1])
    own_dy.start()
    own_x.start()

    barrier = pltpu.get_barrier_semaphore()
    for peer in (other, near_x, near_y):
        pl.semaphore_signal(barrier, inc=1, device_id={'tp': peer}, device_id_type=MESH)
    pl.semaphore_wait(barrier, 3)

    def block(a, owner, c):
        buf, n = ((dy_all, DY_CHUNKS), (x_all, X_CHUNKS))[a]
        w = hidden // n
        return buf.at[pl.ds(pl.multiple_of(owner * ROWS, ROWS), ROWS), pl.ds(c * w, w)]

    recv = ((dy_x, dy_y, dy_d, dy_p), (x_x, x_y, x_d, x_p))

    def copy(a, owner, c, to, kind):
        ref = block(a, owner, c)
        index = 0 if (a == 1 and kind == 3) else c
        return pltpu.make_async_remote_copy(
            src_ref=ref, dst_ref=ref, send_sem=sent.at[a], recv_sem=recv[a][kind].at[index],
            device_id={'tp': to}, device_id_type=MESH)

    def halves(a):
        n = (DY_CHUNKS, X_CHUNKS)[a]
        return list(range(n // 2)), list(range(n // 2, n))

    def send_own(a):
        lo, hi = halves(a)
        for c1, c2 in zip(lo + hi, hi + lo):
            copy(a, me, c1, near_x, 0).start()
            copy(a, me, c2, near_y, 1).start()
        for c in lo + hi:
            copy(a, me, c, other, 3).start()

    def relay_step(a, i):
        lo, hi = halves(a)
        copy(a, near_x, lo[i], other, 0).wait_recv()
        copy(a, near_x, lo[i], near_y, 2).start()
        copy(a, near_x, lo[i], other, 3).start()
        copy(a, near_y, hi[i], other, 1).wait_recv()
        copy(a, near_y, hi[i], near_x, 2).start()
        copy(a, near_y, hi[i], other, 3).start()

    def rest_step(a, i):
        lo, hi = halves(a)
        copy(a, near_x, hi[i], other, 0).wait_recv()
        copy(a, near_x, hi[i], other, 3).start()
        copy(a, near_y, lo[i], other, 1).wait_recv()
        copy(a, near_y, lo[i], other, 3).start()

    def far_step(a, i):
        for part_of in halves(a):
            copy(a, far, part_of[i], other, 2).wait_recv()
            copy(a, far, part_of[i], other, 3).start()

    def elementwise(blocks):
        n = tokens // E_BLOCKS
        for r in blocks:
            s = pl.ds(r * n, n)
            gate = ugu[s, :].astype(F32)
            sig = jax.nn.sigmoid(gate)
            a = gate * sig
            act[s, :] = a
            slope[s, :] = sig * (1.0 + gate * (1.0 - sig))
            z[s, :] = (a * ugu[pl.ds(tokens + r * n, n), :].astype(F32)).astype(BF16)

    get_ug = pltpu.make_async_copy(ug_in, ugu.at[pl.ds(0, tokens), :], load_sem.at[0])
    get_uu = pltpu.make_async_copy(uu_in, ugu.at[pl.ds(tokens, tokens), :], load_sem.at[0])
    get_wd = pltpu.make_async_copy(wd_in, wd, load_sem.at[1])
    get_wg = pltpu.make_async_copy(wg_in, wgu.at[pl.ds(0, hidden), :], load_sem.at[2])
    get_wu = pltpu.make_async_copy(wu_in, wgu.at[pl.ds(hidden, hidden), :], load_sem.at[2])
    own_dy.wait()
    send_own(0)
    for load in (get_ug, get_uu, get_wd, get_wg, get_wu):
        load.start()
    pltpu.make_async_copy(ugu, ugu, load_sem.at[0]).wait()
    elementwise(range(E_BLOCKS - 3))
    own_x.wait()
    relay_step(0, 0)
    relay_step(0, 1)
    send_own(1)
    elementwise(range(E_BLOCKS - 3, E_BLOCKS))
    rest_step(0, 0)
    rest_step(0, 1)
    get_wd.wait()

    def grad_step(c, fresh):
        w = hidden // DY_CHUNKS
        pltpu.make_async_copy(mine_rows(c), mine_rows(c), dy_p.at[c]).wait()
        s = pl.ds(c * w, w)
        term = lax.dot_general(dy_all[:, s], wd[:, s], CONTRACT_COLS, preferred_element_type=F32)
        grad[...] = term if fresh else grad[...] + term

    def mine_rows(c):
        w = hidden // DY_CHUNKS
        return dy_all.at[pl.ds(0, 4 * ROWS), pl.ds(c * w, w)]

    far_step(0, 0)
    grad_step(0, True)
    far_step(0, 1)
    grad_step(2, False)
    grad_step(1, False)
    grad_step(3, False)
    n = tokens // E_BLOCKS
    for r in range(E_BLOCKS):
        s = pl.ds(r * n, n)
        g = grad[s, :]
        duu[s, :] = (g * act[s, :]).astype(BF16)
        dug[s, :] = (g * ugu[pl.ds(tokens + r * n, n), :].astype(F32) * slope[s, :]).astype(BF16)
    pltpu.make_async_copy(wgu, wgu, load_sem.at[2]).wait()

    def give_copy(h):
        s = pl.ds(h * DX_CHUNK, DX_CHUNK)
        return pltpu.make_async_remote_copy(
            src_ref=give.at[:, s], dst_ref=take.at[:, s], send_sem=give_sem.at[0], recv_sem=take_sem.at[h],
            device_id={'tp': other}, device_id_type=MESH)

    def combine(h):
        s = pl.ds(h * DX_CHUNK, DX_CHUNK)
        give_copy(h).wait_recv()
        for ref, device in ((own_out, me), (px_out, near_x), (py_out, near_y), (pd_out, far)):
            d = pl.ds(pl.multiple_of(lax.div(device, 2) * ROWS, ROWS), ROWS)
            ref[:, s] = (mine[d, s] + take[d, s].astype(F32)).astype(BF16)

    for h in range(n_dx):
        s = pl.ds(h * DX_CHUNK, DX_CHUNK)
        part[...] = (lax.dot_general(dug[...], wgu[s, :], CONTRACT_COLS, preferred_element_type=F32)
                     + lax.dot_general(duu[...], wgu[pl.ds(hidden + h * DX_CHUNK, DX_CHUNK), :], CONTRACT_COLS,
                                       preferred_element_type=F32))
        for j in range(4):
            d = pl.ds(j * ROWS, ROWS)
            give[d, s] = part[pl.ds(pl.multiple_of(j * 2 * ROWS + ROWS * (1 - core), ROWS), ROWS), :].astype(BF16)
            mine[d, s] = part[pl.ds(pl.multiple_of(j * 2 * ROWS + ROWS * core, ROWS), ROWS), :]
        give_copy(h).start()
        if h == 0:
            relay_step(1, 0)
        if h == 1:
            rest_step(1, 0)
            combine(0)
    for h in range(1, n_dx):
        combine(h)
    far_step(1, 0)
    pltpu.make_async_copy(give, give, give_sem.at[0]).wait()
    for a, buf in ((0, dy_all), (1, x_all)):
        everything = buf.at[pl.ds(0, 7 * ROWS), :]
        pltpu.make_async_copy(everything, everything, sent.at[a]).wait()
    from_partner = x_all.at[pl.ds(0, 4 * ROWS), :]
    pltpu.make_async_copy(from_partner, from_partner, x_p.at[0]).wait()


def gather_call(x, dy, wg, wu, wd, ug, uu):
    hidden, f = wg.shape
    tokens = ug.shape[0]
    n_dx = hidden // DX_CHUNK
    any_spec = pl.BlockSpec(memory_space=pl.ANY)
    x, dy, wg, wu, wd, ug, uu = [pltpu.with_memory_space_constraint(v, pltpu.HBM) for v in (x, dy, wg, wu, wd, ug, uu)]
    vmem, dma = pltpu.VMEM, pltpu.SemaphoreType.DMA
    full, act, row = vmem((tokens, hidden), BF16), vmem((tokens, f), BF16), vmem((ROWS, hidden), BF16)
    return pl.pallas_call(
        gather_kernel,
        out_shape=(full, full, act, act, act, row, row, row, row),
        in_specs=[any_spec] * 7,
        out_specs=[pl.BlockSpec(memory_space=vmem)] * 9,
        scratch_shapes=[
            vmem((2 * hidden, f), BF16), vmem((f, hidden), BF16), vmem((2 * tokens, f), BF16),
            vmem((tokens, f), F32), vmem((tokens, f), F32), vmem((tokens, f), F32), vmem((tokens, DX_CHUNK), F32),
            vmem((4 * ROWS, hidden), F32), vmem((4 * ROWS, hidden), BF16), vmem((4 * ROWS, hidden), BF16),
            dma((DY_CHUNKS,)), dma((DY_CHUNKS,)), dma((DY_CHUNKS,)), dma((DY_CHUNKS,)),
            dma((X_CHUNKS,)), dma((X_CHUNKS,)), dma((X_CHUNKS,)), dma((1,)),
            dma((2,)), dma((1,)), dma((n_dx,)), dma((2,)), dma((3,)),
        ],
        compiler_params=pltpu.CompilerParams(collective_id=0, has_side_effects=True, vmem_limit_bytes=48 * MIB),
        cost_estimate=pl.CostEstimate(flops=6 * tokens * hidden * f, bytes_accessed=24 * MIB, transcendentals=0),
        name='gather_and_input_grad',
    )(x, dy, wg, wu, wd, ug, uu)


def weight_kernel(x, dy, z, dug, duu, dwg, dwu, dwd):
    xb = x[...]
    dwg[...] = lax.dot_general(xb, dug[...], CONTRACT_ROWS, preferred_element_type=F32)
    dwu[...] = lax.dot_general(xb, duu[...], CONTRACT_ROWS, preferred_element_type=F32)
    dwd[...] = lax.dot_general(z[...], dy[...], CONTRACT_ROWS, preferred_element_type=F32)


def weight_call(x, dy, z, dug, duu, steps=12):
    tokens, hidden = x.shape
    f = z.shape[1]
    h = hidden // steps
    cols = pl.BlockSpec((tokens, h), lambda i: (0, i))
    whole = pl.BlockSpec((tokens, f), lambda i: (0, 0))
    tall = pl.BlockSpec((h, f), lambda i: (i, 0))
    wide = pl.BlockSpec((f, h), lambda i: (0, i))
    return pl.pallas_call(
        weight_kernel,
        grid=(steps,),
        in_specs=[cols, cols, whole, whole, whole],
        out_specs=[tall, tall, wide],
        out_shape=(jax.ShapeDtypeStruct((hidden, f), F32), jax.ShapeDtypeStruct((hidden, f), F32),
                   jax.ShapeDtypeStruct((f, hidden), F32)),
        compiler_params=pltpu.CompilerParams(vmem_limit_bytes=40 * MIB),
        cost_estimate=pl.CostEstimate(flops=6 * tokens * hidden * f, bytes_accessed=42 * MIB, transcendentals=0),
        name='weight_grads',
    )(x, dy, z, dug, duu)


def solution(mesh):
    n = mesh.shape['tp']

    def local_backward(x, wg, wu, wd, ug, uu, dy):
        x_all, dy_all, z, dug, duu, own, px, py, pd = gather_call(x, dy, wg, wu, wd, ug, uu)

        def swap(v, k):
            return lax.ppermute(v, 'tp', [(i, i ^ k) for i in range(n)])

        rx, ry, rd = swap(px, 2), swap(py, 4), swap(pd, 6)
        dwg, dwu, dwd = weight_call(x_all, dy_all, z, dug, duu)
        dx = (own.astype(F32) + rx.astype(F32) + ry.astype(F32) + rd.astype(F32)).astype(BF16)
        return dx, dwg, dwu, dwd

    tok_spec = P(('dp', 'tp'), None)
    col_spec = P(None, 'tp')
    act_spec = P('dp', 'tp')
    return jax.shard_map(local_backward, mesh=mesh,
                         in_specs=(tok_spec, col_spec, col_spec, P('tp', None), act_spec, act_spec, tok_spec),
                         out_specs=(tok_spec, act_spec, act_spec, tok_spec),
                         check_vma=False)
```

time: 108 us -> 40.5 us (0.38)
  Pallas kernels: 0 us -> 35.5 us
  matrix products: 34.8 us -> 0 us
  waiting for transfers between devices: 33.2 us -> 0.01 us
  local copies, waits for them, and re-layouts: 25.5 us -> 0 us
  between operations: 13.8 us -> 0.65 us
  starting transfers between devices: 0.11 us -> 3.51 us
    pallas_call x0 -> x2, Pallas kernels: none -> 35.5 us  [the longest x1 22.5 us: gather_call(): pl.pallas_call(gather_kernel, out_shape=(full, full, act, act, act, row,...]
    dot_general x6 -> x0, matrix products: 34.8 us -> none  [the longest x1 8.02 us: local_backward(): lax.dot_general(x_all, grad_gate, CONTRACT_ROWS, preferred_element_type=j...]
    all_gather x2 -> x0, waiting for transfers between devices: 31.8 us -> none  [the longest x1 23.7 us: local_backward(): dy_all = lax.all_gather(dy_loc, 'tp', axis=0, tiled=True)]
    unnamed x12 -> x0, local copies, waits for them, and re-layouts: 25.5 us -> none
    ppermute x0 -> x3, starting transfers between devices: none -> 3.51 us  [swap(): return lax.ppermute(v, 'tp', [(i, i ^ k) for i in range(n)])]
    unnamed x3 -> x0, waiting for transfers between devices: 1.39 us -> none
  transfers between devices with their start and end apart: 3 -> 3, of which waited for: 2 -> 0; matrix products, arithmetic and copies ran while one was open for 56% -> 0% of each run, Pallas kernels for 0% -> 32%
where the time goes in v3:
time: 40.5 us; the launch traced here: 40.4 us
  Pallas kernels  35.5 us (88%)
  starting transfers between devices  3.51 us (9%)
  other arithmetic  0.78 us (2%)
  between operations  0.65 us (2%)
    pallas_call x1, Pallas kernels, gather_call(): pl.pallas_call(gather_kernel, out_shape=(full, full, act, act, act, row,...  22.5 us
    pallas_call x1, Pallas kernels, weight_call(): pl.pallas_call(weight_kernel, grid=(steps,), in_specs=[cols, cols, whole,...  13 us
    ppermute x3, starting transfers between devices, swap(): return lax.ppermute(v, 'tp', [(i, i ^ k) for i in range(n)])  3.51 us
  transfers between devices with their start and end apart: 3, of which 0 were waited for; matrix products, arithmetic and copies ran while one was open for 0% of the time, Pallas kernels for 32%

profile of v3, /device:TPU:0, one launch (start us, length us, event | category | flops | bytes accessed | tf_op | source)
XLA Modules:
  0.0 40.4 jit_solution(8604870396308692352)
XLA Ops:
  0.6 22.5 %gather_and_input_grad.1 = (bf16[256,3072]{1,0:T(8,128)(2,1)S(1)}, bf16[256,3072]{1,0:T(8,128)(2,1)S(1)}, bf16[256,1024]{1,0:T(8,128)(2,1)S(1)}, bf16[256,1024]{...) custom-call(bf16[32,3072]{1,0:T(8,128)(2,1)} %x_in.1, ...), custom_call_target="tpu_custom_call" | custom-call | flops 4831838208 | bytes 25165824 | tf_op jit(solution)/shard_map/gather_and_input_grad/pallas_call | solution.py:200
  23.1 0.9 %collective-permute-start = (bf16[32,3072]{1,0:T(8,128)(2,1)S(1)}, bf16[32,3072]{1,0:T(8,128)(2,1)S(1)}, u32[]{:S(2)}, u32[]{:S(2)}) collective-permute-start(bf16[32,3072]{1,0:T(8,128)(2,1)S(1)} %get-tuple-element.17), channel_id=1, source_target_pairs={{0,2},{1,3},{2,0},{3,1},{4,6},{5,7},{6,4},{7,5}} | collective-permute-start | bytes 589832 | tf_op jit(solution)/shard_map/ppermute | solution.py:254
  24.1 1.1 %collective-permute-start.1 = (bf16[32,3072]{1,0:T(8,128)(2,1)S(1)}, bf16[32,3072]{1,0:T(8,128)(2,1)S(1)}, u32[]{:S(2)}, u32[]{:S(2)}) collective-permute-start(bf16[32,3072]{1,0:T(8,128)(2,1)S(1)} %get-tuple-element.18), channel_id=1, source_target_pairs={{0,4},{1,5},{2,6},{3,7},{4,0},{5,1},{6,2},{7,3}} | collective-permute-start | bytes 589832 | tf_op jit(solution)/shard_map/ppermute | solution.py:254
  25.2 1.5 %collective-permute-start.2 = (bf16[32,3072]{1,0:T(8,128)(2,1)S(1)}, bf16[32,3072]{1,0:T(8,128)(2,1)S(1)}, u32[]{:S(2)}, u32[]{:S(2)}) collective-permute-start(bf16[32,3072]{1,0:T(8,128)(2,1)S(1)} %get-tuple-element.19), channel_id=1, source_target_pairs={{0,6},{1,7},{2,4},{3,5},{4,2},{5,3},{6,0},{7,1}} | collective-permute-start | bytes 589832 | tf_op jit(solution)/shard_map/ppermute | solution.py:254
  26.7 13.0 %weight_grads.1 = (f32[3072,1024]{1,0:T(8,128)}, f32[3072,1024]{1,0:T(8,128)}, f32[1024,3072]{1,0:T(8,128)}) custom-call(bf16[256,3072]{1,0:T(8,128)(2,1)S(1)} %get-tuple-element.20.x, bf16[256,3072]{1,0:T(8,128)(2,1)S(1)} %get-tuple-element.21.dy, bf16[256,1024]{1,0:T(8,128)(2,1)S(1)} %get-tuple-element.22.z, bf16[256,1024]{1,0:T(8,128)(2,1)S(1)} %get-tuple-element.23.dug, ...), custom_call_target="tpu_custom_call" | custom-call | flops 4831838208 | bytes 44040192 | tf_op jit(solution)/shard_map/weight_grads/pallas_call | solution.py:234
  39.6 0.0 collective-permute-done
  39.6 0.0 collective-permute-done.1
  39.6 0.0 collective-permute-done.2
  39.6 0.8 %add_convert_fusion = bf16[32,3072]{1,0:T(8,128)(2,1)} fusion(bf16[32,3072]{1,0:T(8,128)(2,1)S(1)} %collective-permute-done.2, bf16[32,3072]{1,0:T(8,128)(2,1)S(1)} %collective-permute-done.1, bf16[32,3072]{1,0:T(8,128)(2,1)S(1)} %collective-permute-done, bf16[32,3072]{1,0:T(8,128)(2,1)S(1)} %get-tuple-element.16), kind=kLoop, calls=%fused_computation | loop fusion | flops 786432 | bytes 983040 | tf_op jit(solution)/shard_map/convert_element_type | solution.py:258
Async XLA Ops:
  23.1 16.5 %collective-permute-start = (bf16[32,3072]{1,0:T(8,128)(2,1)S(1)}, bf16[32,3072]{1,0:T(8,128)(2,1)S(1)}, u32[]{:S(2)}, u32[]{:S(2)}) collective-permute-start(bf16[32,3072]{1,0:T(8,128)(2,1)S(1)} %get-tuple-element.17), channel_id=1, source_target_pairs={{0,2},{1,3},{2,0},{3,1},{4,6},{5,7},{6,4},{7,5}} | collective-permute-start | bytes 589832 | tf_op jit(solution)/shard_map/ppermute | solution.py:254
  24.1 15.6 %collective-permute-start.1 = (bf16[32,3072]{1,0:T(8,128)(2,1)S(1)}, bf16[32,3072]{1,0:T(8,128)(2,1)S(1)}, u32[]{:S(2)}, u32[]{:S(2)}) collective-permute-start(bf16[32,3072]{1,0:T(8,128)(2,1)S(1)} %get-tuple-element.18), channel_id=1, source_target_pairs={{0,4},{1,5},{2,6},{3,7},{4,0},{5,1},{6,2},{7,3}} | collective-permute-start | bytes 589832 | tf_op jit(solution)/shard_map/ppermute | solution.py:254
  25.2 14.5 %collective-permute-start.2 = (bf16[32,3072]{1,0:T(8,128)(2,1)S(1)}, bf16[32,3072]{1,0:T(8,128)(2,1)S(1)}, u32[]{:S(2)}, u32[]{:S(2)}) collective-permute-start(bf16[32,3072]{1,0:T(8,128)(2,1)S(1)} %get-tuple-element.19), channel_id=1, source_target_pairs={{0,6},{1,7},{2,4},{3,5},{4,2},{5,3},{6,0},{7,1}} | collective-permute-start | bytes 589832 | tf_op jit(solution)/shard_map/ppermute | solution.py:254
